TPU v7x, 256 devices: a 2x2x32 block of a 4x8x32 slice. The times are simulated.
256 devices in a mesh: parts: 4 (over x, y), owner: 64 (over z, core).
Axes of the slice: x: 2, y: 2, z: 32, core: 2. Of those that a mesh axis runs over, the one named last changes fastest.
The devices are a block of a 4x8x32 slice.
Arguments:
- embeddings: bfloat16 [262144, 768], P(('parts', 'owner')), parts along dimension 0, may hold values from -6 to 6
- cluster_ids: int32 [262144], P(('parts', 'owner')), parts along dimension 0, may hold values from 0 to 255, as said below
- owner_map: int32 [1024], P('parts'), parts along dimension 0, may hold values from 0 to 63, as said below
Outputs:
- maxima: float32 [262144], P(('parts', 'owner')), parts along dimension 0
- cluster_mean: float32 [1024], P('parts'), parts along dimension 0
There are 4 independent parts, one for each index of `parts`. A program takes and returns all parts, laid end to end along the dimension named above; each array names one. Nothing has to cross between parts.
Inputs may be any that keep to these rules, and one draw needn't show every extreme that they name: `cluster_ids`: cluster of each item. Owners 2k and 2k+1 form a pair; exactly 32 of the items of one device belong to clusters of one pair, so at most 32 to one owner, and in every draw some owner receives exactly 32 items from every device. `owner_map`: every owner owns exactly 4 clusters.
All inputs are finite; a program needn't handle non-finite values.
Results may differ from a plain program's by a relative error of at most 0.0015.
Values may be sent and summed in bfloat16 or wider, within the bound.
A program may use at most 64 MiB of HBM per device.

v0:
```python
import math

import jax
import jax.numpy as jnp
from jax import lax
from jax.sharding import PartitionSpec as P


def partner(value, axis, bit):
    mask = 2**bit
    pairs = [(source, source ^ mask) for source in range(lax.axis_size(axis))]
    return lax.ppermute(value, axis, pairs)


def copy_for_each(value, axis):
    length = lax.axis_size(axis)
    return lax.all_to_all(
        jnp.broadcast_to(value[None], (length, *value.shape)), axis, 0, 0, tiled=True
    )


def taken_together(value, axis):
    return copy_for_each(value, axis).sum(axis=0)


def in_one(arrays, axis):
    ends = [0]
    for a in arrays:
        ends.append(ends[-1] + a.size)
    subtotal = taken_together(jnp.concatenate([a.ravel() for a in arrays]), axis)
    return tuple((subtotal[b:e].reshape(a.shape) for a, b, e in zip(arrays, ends, ends[1:])))


def unitize(rows):
    values = rows.astype(jnp.float32)
    scale = lax.rsqrt(jnp.mean(values * values, axis=-1, keepdims=True) + 1e-06)
    return (values * scale / jnp.sqrt(jnp.float32(values.shape[-1]))).astype(jnp.bfloat16)


def rows_against(queries, query_labels, keys, key_labels):
    total = queries.shape[0]
    width = math.gcd(total, 512)
    blocks = total // width
    columns = jnp.arange(keys.shape[0], dtype=jnp.int32)
    pieces = []
    for first in range(blocks):
        gram = jnp.dot(
            queries[first * width : (first + 1) * width], keys.T, preferred_element_type=jnp.float32
        )
        left = query_labels[first * width : (first + 1) * width]
        rows = first * width + jnp.arange(width, dtype=jnp.int32)
        mask = (
            (left[:, None] == key_labels[None, :])
            & (left[:, None] >= 0)
            & (rows[:, None] != columns[None, :])
        )
        pieces.append(jnp.max(jnp.where(mask, gram, jnp.float32(-1.0)), axis=1))
    return jnp.concatenate(pieces)


def body(embeddings, cluster_ids, owner_map):
    owners = lax.axis_size("owner")
    items = embeddings.shape[0]
    width = embeddings.shape[1]
    clusters = owner_map.shape[0]
    capacity = 2 * items // owners
    cluster_range = jnp.arange(clusters, dtype=jnp.int32)
    hits = cluster_ids[:, None] == cluster_range[None, :]
    owner_of = jnp.sum(jnp.where(hits, owner_map[None, :], 0), axis=1)
    half = capacity // 2
    slot_total = owners * half
    pair_of = owner_of // 2
    pair_hot = (pair_of[:, None] == jnp.arange(owners // 2, dtype=jnp.int32)[None, :]).astype(
        jnp.int32
    )
    pair_rank = jnp.sum(jnp.cumsum(pair_hot, axis=0) * pair_hot, axis=1) - 1
    target = 2 * pair_of + pair_rank % 2
    slot = target * half + pair_rank // 2
    send_rows = jnp.zeros((slot_total, width), jnp.bfloat16).at[slot].set(embeddings)
    send_labels = jnp.full((slot_total,), -1, jnp.int32).at[slot].set(cluster_ids)
    arrived = lax.all_to_all(send_rows, "owner", split_axis=0, concat_axis=0, tiled=True)
    labels = lax.all_to_all(send_labels, "owner", split_axis=0, concat_axis=0, tiled=True)
    unit = unitize(arrived)
    partner_unit, partner_labels = partner((unit, labels), "owner", 0)
    keys = jnp.concatenate([unit, partner_unit], axis=0)
    key_labels = jnp.concatenate([labels, partner_labels], axis=0)
    best = rows_against(unit, labels, keys, key_labels)
    returned = lax.all_to_all(best, "owner", split_axis=0, concat_axis=0, tiled=True)
    maxima = returned[slot]
    member = labels[:, None] == cluster_range[None, :]
    sums = jnp.sum(jnp.where(member, best[:, None], 0.0), axis=0)
    counts = jnp.sum(member.astype(jnp.float32), axis=0)
    totals, numbers = in_one((sums, counts), "owner")
    return (maxima, totals / jnp.maximum(numbers, 1.0))


def solution(mesh):
    placed = (P(("parts", "owner"), None), P(("parts", "owner")), P("parts"))
    return jax.shard_map(
        body,
        mesh=mesh,
        in_specs=placed,
        out_specs=(P(("parts", "owner")), P("parts")),
        check_vma=False,
    )
```

profile of v0, /device:TPU:37, one launch (start us, length us, event | category | flops | bytes accessed | tf_op | source)
XLA Modules:
  0.0 315.7 jit_solution(15345792976544001412)
XLA Ops:
  0.6 1.1 select_reduce_fusion.3
  1.7 9.0 %reduce-window.6 = s32[32,8,128]{2,1,0:T(8,128)S(1)} reduce-window(s32[32,8,128]{2,1,0:T(8,128)S(1)} %fusion.10, s32[]{:T(128)} %constant.54.clone.1), window={size=1x1x128 pad=0_0x0_0x127_0}, to_apply=%region_1.2 | reduce-window | flops 4161536 | bytes 262148 | tf_op jit(solution)/shard_map/reduce-window
  10.8 0.1 slice.36
  10.9 0.1 copy.17
  11.0 0.1 copy.18
  11.1 0.1 broadcast_add_fusion
  11.3 0.1 compare_select_fusion
  11.3 6.2 %scatter_custom_fusion.1 = bf16[1024,768]{1,0:T(8,128)(2,1)S(1)} fusion(s32[1024]{0:T(1024)S(1)} %bitcast.50, bf16[1024,768]{1,0:T(8,128)(2,1)} %param.3, bf16[]{:T(256)} %constant.59.clone.1), kind=kCustom, calls=%fused_computation.21 | custom fusion | bytes 1573376 | tf_op jit(solution)/shard_map/scatter | solution.py:79
  17.6 187.0 %all_to_all.36 = bf16[64,16,768]{2,1,0:T(8,128)(2,1)S(1)} all-to-all(bf16[64,16,768]{2,1,0:T(8,128)(2,1)S(1)} %bitcast.46), channel_id=1, replica_groups=mesh['parts'=4,'owner'=64] {'owner'}, dimensions={0} | all-to-all | bytes 3145728 | tf_op jit(solution)/shard_map/all_to_all | solution.py:81
  204.5 0.4 multiply_reduce_fusion
  204.9 0.1 rsqrt.12
  205.0 0.4 fusion.3
  205.4 2.7 collective-permute-start.1
  208.1 4.5 %scatter_custom_fusion = s32[1024]{0:T(1024)S(1)} fusion(s32[1024]{0:T(1024)S(1)} %bitcast.51, s32[1024]{0:T(1024)} %param.4, s32[]{:T(128)} %constant.53.clone.1), kind=kCustom, calls=%fused_computation.66 | custom fusion | bytes 4608 | tf_op jit(solution)/shard_map/scatter | solution.py:80
  212.6 0.7 all_to_all.24
  213.3 5.1 %all-to-all-start = ((s32[64,16,1]{1,2,0:T(1,128)}), s32[64,16,1]{1,2,0:T(1,128)S(1)}, u32[]{:S(2)}, u32[]{:S(2)}) async-start(s32[64,16,1]{1,2,0:T(1,128)} %bitcast.6), calls=%async_computation | async-start | bytes 65536 | tf_op jit(solution)/shard_map/all_to_all | solution.py:82
  218.5 22.6 %all-to-all-done = s32[64,16,1]{1,2,0:T(1,128)S(1)} async-done(((s32[64,16,1]{1,2,0:T(1,128)}), s32[64,16,1]{1,2,0:T(1,128)S(1)}, u32[]{:S(2)}, u32[]{:S(2)}) %all-to-all-start) | async-done | bytes 4128 | tf_op jit(solution)/shard_map/all_to_all | solution.py:82
  241.1 0.5 broadcast.282
  241.6 0.7 reduce.16
  242.3 0.1 all_to_all.26
  242.4 0.1 slice_reduce_fusion.1
  242.5 0.1 eq.86
  242.5 0.1 eq.90
  242.6 1.0 collective-permute-start
  243.6 0.8 collective-permute-done
  244.4 0.0 collective-permute-done.1
  244.4 2.1 select_reduce_fusion.1
  246.5 0.1 concatenate.21
  246.6 2.4 select_reduce_fusion
  249.0 0.1 concatenate.22
  249.1 0.4 select_reduce_fusion.2
  249.5 0.6 pad_maximum_fusion.3
  250.1 5.2 %all-to-all-start.2 = ((f32[64,16,1]{1,2,0:T(1,128)}), f32[64,16,1]{1,2,0:T(1,128)S(1)}, u32[]{:S(2)}, u32[]{:S(2)}) async-start(f32[64,16,1]{1,2,0:T(1,128)} %bitcast.9), calls=%async_computation.2 | async-start | bytes 65536 | tf_op jit(solution)/shard_map/all_to_all | solution.py:88
  255.3 22.7 %all-to-all-done.2 = f32[64,16,1]{1,2,0:T(1,128)S(1)} async-done(((f32[64,16,1]{1,2,0:T(1,128)}), f32[64,16,1]{1,2,0:T(1,128)S(1)}, u32[]{:S(2)}, u32[]{:S(2)}) %all-to-all-start.2) | async-done | bytes 4128 | tf_op jit(solution)/shard_map/all_to_all | solution.py:88
  278.0 0.7 broadcast_in_dim.42
  278.7 5.7 %all-to-all-start.3 = ((f32[64,1,512]{2,1,0:T(1,128)}), f32[64,1,512]{2,1,0:T(1,128)S(1)}, u32[]{:S(2)}, u32[]{:S(2)}) async-start(f32[64,1,512]{2,1,0:T(1,128)} %broadcast_in_dim.42), calls=%async_computation.3 | async-start | bytes 262144 | tf_op jit(solution)/shard_map/all_to_all | solution.py:17
  284.4 0.5 broadcast.283
  285.0 0.7 reduce.17
  285.7 0.1 all_to_all.30
  285.8 8.8 %gather_fusion = f32[1024]{0:T(1024)} fusion(f32[1024]{0:T(1024)S(1)} %all_to_all.30, s32[1024]{0:T(1024)S(1)} %broadcast_clamp_fusion), kind=kCustom, calls=%fused_computation | custom fusion | bytes 12288 | tf_op jit(solution)/shard_map/gather | solution.py:89
  294.6 20.4 %all-to-all-done.3 = f32[64,1,512]{2,1,0:T(1,128)S(1)} async-done(((f32[64,1,512]{2,1,0:T(1,128)}), f32[64,1,512]{2,1,0:T(1,128)S(1)}, u32[]{:S(2)}, u32[]{:S(2)}) %all-to-all-start.3) | async-done | bytes 131104 | tf_op jit(solution)/shard_map/all_to_all | solution.py:17
  315.0 0.1 reduce_sum.65
  315.1 0.6 maximum_divide_fusion
  (15 shorter events, 0.2 us)
Async XLA Ops:
  205.4 39.0 %collective-permute-start.1 = (bf16[1024,768]{1,0:T(8,128)(2,1)S(1)}, bf16[1024,768]{1,0:T(8,128)(2,1)S(1)}, u32[]{:S(2)}, u32[]{:S(2)}) collective-permute-start(bf16[1024,768]{1,0:T(8,128)(2,1)S(1)} %fusion.3), channel_id=1, source_target_pairs={{0,1},{1,0},{2,3},{3,2},{4,5},{5,4},{6,7},{7,6},{8,9},{9,8},{10,11... | collective-permute-start | bytes 4718600 | tf_op jit(solution)/shard_map/ppermute | solution.py:12
  213.3 27.8 %all-to-all-start = ((s32[64,16,1]{1,2,0:T(1,128)}), s32[64,16,1]{1,2,0:T(1,128)S(1)}, u32[]{:S(2)}, u32[]{:S(2)}) async-start(s32[64,16,1]{1,2,0:T(1,128)} %bitcast.6), calls=%async_computation | async-start | bytes 65536 | tf_op jit(solution)/shard_map/all_to_all | solution.py:82
  242.6 1.8 collective-permute-start
  250.1 27.9 %all-to-all-start.2 = ((f32[64,16,1]{1,2,0:T(1,128)}), f32[64,16,1]{1,2,0:T(1,128)S(1)}, u32[]{:S(2)}, u32[]{:S(2)}) async-start(f32[64,16,1]{1,2,0:T(1,128)} %bitcast.9), calls=%async_computation.2 | async-start | bytes 65536 | tf_op jit(solution)/shard_map/all_to_all | solution.py:88
  278.7 36.3 %all-to-all-start.3 = ((f32[64,1,512]{2,1,0:T(1,128)}), f32[64,1,512]{2,1,0:T(1,128)S(1)}, u32[]{:S(2)}, u32[]{:S(2)}) async-start(f32[64,1,512]{2,1,0:T(1,128)} %broadcast_in_dim.42), calls=%async_computation.3 | async-start | bytes 262144 | tf_op jit(solution)/shard_map/all_to_all | solution.py:17
where the time goes:
time: 316 us
  blocking collectives  187 us (59%)
  waiting for transfers between devices  66.6 us (21%)
  local copies, waits for them, and re-layouts  22.8 us (7%)
  starting transfers between devices  19.7 us (6%)
  other arithmetic  14.3 us (5%)
  matrix products  4.5 us (1%)
    all_to_all x1, blocking collectives, body(): lax.all_to_all(send_rows, 'owner', split_axis=0, concat_axis=0, tiled=True)  187 us
    all_to_all x1, waiting for transfers between devices, body(): lax.all_to_all(best, 'owner', split_axis=0, concat_axis=0, tiled=True)  22.7 us
    all_to_all x1, waiting for transfers between devices, body(): lax.all_to_all(send_labels, 'owner', split_axis=0, concat_axis=0, tiled=T...  22.6 us
    all_to_all x1, waiting for transfers between devices, copy_for_each(): lax.all_to_all(jnp.broadcast_to(value[None], (length, *value.shape)), axi...  20.4 us
    another operation x3, other arithmetic  9.15 us
    gather x1, local copies, waits for them, and re-layouts, body(): maxima = returned[slot]  8.83 us
  transfers between devices with their start and end apart: 5, of which 4 were waited for; matrix products, arithmetic and copies ran while one was open for 5% of the time, Pallas kernels for 0%

commit v1 on v0

v1 whole, which is shorter than its diff:
```python
import functools
import math

import jax
import jax.numpy as jnp
from jax import lax
from jax.experimental import pallas as pl
from jax.experimental.pallas import tpu as pltpu
from jax.sharding import PartitionSpec as P

MESH = pl.DeviceIdType.MESH
LANES = 128
GROUPS = ((0, 16), (16, 24), (24, 28), (28, 32))
NT = (((1,), (1,)), ((), ()))
TN = (((0,), (0,)), ((), ()))


def iota(shape, dim):
    return lax.broadcasted_iota(jnp.int32, shape, dim)


def upto(n):
    return jnp.where(iota((n, n), 0) <= iota((n, n), 1), 1.0, 0.0).astype(jnp.bfloat16)


def product(a, b, dims=(((1,), (0,)), ((), ()))):
    return lax.dot_general(a, b, dims, preferred_element_type=jnp.float32)


def delta_of(pos, chips):
    if pos == 0:
        return 0
    return (chips + 1 - pos) // 2 if pos % 2 else (pos + chips) // 2


def place_of(delta, chips):
    ahead = jnp.where(delta <= chips // 2, chips + 1 - 2 * delta, 2 * delta - chips)
    return jnp.where(delta == 0, 0, ahead)


def three_parts(x):
    high = x.astype(jnp.bfloat16)
    rest = x - high.astype(jnp.float32)
    middle = rest.astype(jnp.bfloat16)
    low = (rest - middle.astype(jnp.float32)).astype(jnp.bfloat16)
    return high, middle, low


def kernel(
    chips, ids_ref, map_ref, rows_ref, max_ref, mean_ref,
    send, keys, lab_s, lab_r, lab_q, lab_k, acc, ret_s, ret_r, mp_s, mp_r, place, lane_at,
    data_ss, data_rs, lab_ss, lab_rs, fwd_ss, fwd_rs, ret_ss, ret_rs, two_ss, two_rs,
):
    items, width = rows_ref.shape
    clusters = map_ref.shape[1]
    block = items // chips
    per = LANES // block
    me = lax.axis_index("owner")
    core, z = lax.rem(me, 2), me // 2
    partner = {"owner": z * 2 + 1 - core}

    def chip(delta):
        return {"owner": lax.rem(z + delta + 2 * chips, chips) * 2 + core}

    barrier = pltpu.get_barrier_semaphore()
    for pos in range(1, chips):
        pl.semaphore_signal(barrier, inc=1, device_id=chip(delta_of(pos, chips)), device_id_type=MESH)
    pl.semaphore_signal(barrier, inc=1, device_id=partner, device_id_type=MESH)

    pair_c = lax.shift_right_logical(map_ref[...], 1)
    place_c = place_of(lax.rem(pair_c - z + chips, chips), chips)
    at_c = jnp.where(iota((chips, clusters), 0) == place_c, 1.0, 0.0)
    count_c = product(at_c.astype(jnp.bfloat16), upto(clusters))
    local_c = jnp.sum(at_c * count_c, axis=0, keepdims=True) - 1.0

    hits = jnp.where(iota((clusters, items), 0) == ids_ref[...], 1.0, 0.0).astype(jnp.bfloat16)
    table = jnp.concatenate([at_c, jnp.broadcast_to(local_c, (16, clusters))], axis=0).astype(jnp.bfloat16)
    found = product(table, hits)
    at = found[:chips]
    label = found[chips:].astype(jnp.bfloat16)
    tiles = items // LANES
    stacked = jnp.concatenate([at[:, t * LANES : (t + 1) * LANES] for t in range(tiles)], axis=0)
    sums = product(stacked.astype(jnp.bfloat16), upto(LANES))
    row = iota((chips, LANES), 0).astype(jnp.float32)
    before = jnp.zeros((chips, 1), jnp.float32)
    places, slots = [], []
    for t in range(tiles):
        at_t = stacked[t * chips : (t + 1) * chips]
        sum_t = sums[t * chips : (t + 1) * chips]
        places.append(jnp.sum(at_t * row, axis=0, keepdims=True))
        slots.append(jnp.sum(at_t * (sum_t + before + row * block), axis=0, keepdims=True) - 1.0)
        before = before + sum_t[:, LANES - 1 :]
    place_i = jnp.concatenate(places, axis=1).astype(jnp.int32)
    slot = jnp.concatenate(slots, axis=1).astype(jnp.int32)
    place[:, :items] = place_i
    place[:, items:] = place_c
    lane_at[:, :items] = lax.rem(slot, LANES)
    lane_at[:, items:] = lax.rem(place_c + 1, per) * block + local_c.astype(jnp.int32)

    def data_copy(pos):
        return pltpu.make_async_remote_copy(
            src_ref=send.at[pl.ds(pos * block, block)], dst_ref=keys.at[pl.ds(pos * block, block)],
            send_sem=data_ss.at[pos], recv_sem=data_rs.at[pos],
            device_id=chip(delta_of(pos, chips)), device_id_type=MESH,
        )

    def label_copy(pos):
        return pltpu.make_async_remote_copy(
            src_ref=lab_s.at[pos // per], dst_ref=lab_r.at[pos],
            send_sem=lab_ss.at[pos], recv_sem=lab_rs.at[pos],
            device_id=chip(delta_of(pos, chips)), device_id_type=MESH,
        )

    def forward_copy(pos):
        return pltpu.make_async_remote_copy(
            src_ref=keys.at[pl.ds(pos * block, block)], dst_ref=keys.at[pl.ds(items + pos * block, block)],
            send_sem=fwd_ss.at[pos], recv_sem=fwd_rs.at[pos], device_id=partner, device_id_type=MESH,
        )

    def return_copy(pos):
        return pltpu.make_async_remote_copy(
            src_ref=ret_s.at[pos], dst_ref=ret_r.at[pos],
            send_sem=ret_ss.at[pos], recv_sem=ret_rs.at[pos],
            device_id=chip(-delta_of(pos, chips)), device_id_type=MESH,
        )

    labels_over = pltpu.make_async_remote_copy(
        src_ref=lab_r.at[pl.ds(0, chips)], dst_ref=lab_r.at[pl.ds(chips, chips)],
        send_sem=two_ss.at[0], recv_sem=two_rs.at[0], device_id=partner, device_id_type=MESH,
    )
    means_over = pltpu.make_async_remote_copy(
        src_ref=mp_s, dst_ref=mp_r,
        send_sem=two_ss.at[1], recv_sem=two_rs.at[1], device_id=partner, device_id_type=MESH,
    )

    step = 2 * LANES
    for first in range(0, items, step):
        pick = jnp.where(iota((step, items), 0) + first == slot, 1.0, 0.0).astype(jnp.bfloat16)
        rows = product(pick, rows_ref[...])
        scale = lax.rsqrt(jnp.mean(rows * rows, axis=1, keepdims=True) + 1e-06)
        unit = (rows * scale * jnp.float32(width**-0.5)).astype(jnp.bfloat16)
        send[first : first + step] = unit
        names = product(label, pick, NT)
        for t in range(step // LANES):
            lab_s[first // LANES + t] = names[:1, t * LANES : (t + 1) * LANES]
        if first == 0:
            keys[:block] = unit[:block]
            lab_r[0] = names[:1, :LANES]
            pl.semaphore_wait(barrier, chips)
        for pos in range(first // block, (first + step) // block):
            if pos > 0:
                data_copy(pos).start()
                label_copy(pos).start()
    forward_copy(0).start()

    for pos in range(1, chips):
        label_copy(pos).wait_recv()
    labels_over.start()
    labels_over.wait_recv()
    quarter = lax.div(iota((1, LANES), 1), block)
    for t in range(2 * tiles):
        mixed = jnp.zeros((1, LANES), jnp.float32)
        for q in range(per):
            mixed = jnp.where(quarter == q, lab_r[t * per + q], mixed)
        lab_q[:, t * LANES : (t + 1) * LANES] = mixed
        lab_k[t * LANES : (t + 1) * LANES] = jnp.broadcast_to(mixed, (LANES, LANES)).T
    acc[...] = jnp.full(acc.shape, -1.0, jnp.float32)

    def meet(k0, kn, q0, qn, own):
        gram = product(keys[pl.ds(k0, kn)], keys[q0 : q0 + qn], NT)
        same = jnp.concatenate([lab_k[pl.ds(k0, kn)]] * (qn // LANES), axis=1) == lab_q[:, q0 : q0 + qn]
        if own:
            same = same & (iota((kn, qn), 0) + k0 != iota((kn, qn), 1) + q0)
        best = jnp.where(same, gram, -1.0)
        acc[:, q0 : q0 + qn] = jnp.maximum(acc[:, q0 : q0 + qn], jnp.max(best.reshape(kn // 8, 8, qn), axis=0))

    def meet_all(k0, kn, q0, qn, own):
        size = math.gcd(kn, 2 * LANES)
        if kn == size:
            meet(k0, kn, q0, qn, own)
        else:
            @pl.loop(0, kn // size)
            def _(i):
                meet(pl.multiple_of(k0 + i * size, LANES), size, q0, qn, own)

    for low, high in GROUPS:
        for pos in range(low, high):
            if pos > 0:
                data_copy(pos).wait_recv()
                forward_copy(pos).start()
        for pos in range(low, high):
            forward_copy(pos).wait_recv()
        old, new, end = low * block, (high - low) * block, high * block
        meet_all(old, new, 0, end, True)
        meet_all(items + old, new, 0, end, False)
        if old:
            meet_all(0, old, old, new, False)
            meet_all(items, old, old, new, False)

    best = jnp.max(acc[...], axis=0, keepdims=True)
    kinds = 8
    kind = iota((kinds, items), 0).astype(jnp.float32)
    mine = jnp.where(kind == lab_q[:, :items], 1.0, 0.0)
    other = jnp.where(kind == lab_q[:, items:], 1.0, 0.0)
    numbers = jnp.sum(mine + other, axis=1, keepdims=True)
    part = jnp.sum(mine * best, axis=1, keepdims=True) / jnp.maximum(numbers, 1.0)
    spread = jnp.where(iota((kinds, LANES), 0) == lax.rem(iota((kinds, LANES), 1), kinds), part, 0.0)
    parts = jnp.sum(spread, axis=0, keepdims=True)
    for pos in range(chips):
        first = pos // per * LANES
        packed = jnp.where(quarter == pos % per, best[:, first : first + LANES], parts)
        if pos == 0:
            ret_r[0] = packed
        else:
            ret_s[pos] = packed
    for pos in range(1, chips):
        return_copy(pos).start()

    for pos in range(chips):
        if pos > 0:
            data_copy(pos).wait_send()
            label_copy(pos).wait_send()
        forward_copy(pos).wait_send()
    labels_over.wait_send()
    total = items + clusters
    here = jnp.where(iota((chips, total), 0) == place[...], 1.0, 0.0).astype(jnp.bfloat16)
    here = jnp.concatenate([here] * 3, axis=0)
    wanted = iota((LANES, total), 0) == lane_at[...]
    for pos in range(1, chips):
        return_copy(pos).wait_recv()
    back = jnp.concatenate([ret_r[pos] for pos in range(chips)], axis=0)
    values = product(jnp.concatenate(three_parts(back), axis=0), here, TN)
    out = jnp.sum(jnp.where(wanted, values, 0.0), axis=0, keepdims=True)
    mp_s[...] = out[:, items:]
    means_over.start()
    max_ref[...] = out[:, :items]
    for pos in range(1, chips):
        return_copy(pos).wait_send()
    means_over.wait()
    mean_ref[...] = mp_s[...] + mp_r[...]


def body(embeddings, cluster_ids, owner_map):
    chips = lax.axis_size("owner") // 2
    items, width = embeddings.shape
    clusters = owner_map.shape[0]
    vmem = pl.BlockSpec(memory_space=pltpu.VMEM)
    row = (1, LANES)
    copies = [pltpu.SemaphoreType.DMA((chips,))] * 2
    maxima, means = pl.pallas_call(
        functools.partial(kernel, chips),
        out_shape=(
            jax.ShapeDtypeStruct((1, items), jnp.float32),
            jax.ShapeDtypeStruct((1, clusters), jnp.float32),
        ),
        in_specs=[vmem] * 3,
        out_specs=(vmem, vmem),
        scratch_shapes=[
            pltpu.VMEM((items, width), jnp.bfloat16),
            pltpu.VMEM((2 * items, width), jnp.bfloat16),
            pltpu.VMEM((items // LANES, *row), jnp.float32),
            pltpu.VMEM((2 * chips, *row), jnp.float32),
            pltpu.VMEM((1, 2 * items), jnp.float32),
            pltpu.VMEM((2 * items, LANES), jnp.float32),
            pltpu.VMEM((8, items), jnp.float32),
            pltpu.VMEM((chips, *row), jnp.float32),
            pltpu.VMEM((chips, *row), jnp.float32),
            pltpu.VMEM((1, clusters), jnp.float32),
            pltpu.VMEM((1, clusters), jnp.float32),
            pltpu.VMEM((1, items + clusters), jnp.int32),
            pltpu.VMEM((1, items + clusters), jnp.int32),
            *copies, *copies, *copies, *copies,
            *[pltpu.SemaphoreType.DMA((2,))] * 2,
        ],
        compiler_params=pltpu.CompilerParams(collective_id=0, has_side_effects=True),
    )(cluster_ids.reshape(1, items), owner_map.reshape(1, clusters), embeddings)
    return maxima.reshape(items), means.reshape(clusters)


def solution(mesh):
    placed = (P(("parts", "owner"), None), P(("parts", "owner")), P("parts"))
    return jax.shard_map(
        body,
        mesh=mesh,
        in_specs=placed,
        out_specs=(P(("parts", "owner")), P("parts")),
        check_vma=False,
    )
```

time: 316 us -> 210 us (0.66)
  Pallas kernels: 0 us -> 207 us
  blocking collectives: 187 us -> 0 us
  waiting for transfers between devices: 66.6 us -> 0 us
  local copies, waits for them, and re-layouts: 22.8 us -> 2.48 us
  starting transfers between devices: 19.7 us -> 0 us
  other arithmetic: 14.3 us -> 0 us
  matrix products: 4.5 us -> 0 us
    pallas_call x0 -> x1, Pallas kernels: none -> 207 us  [body(): pl.pallas_call(functools.partial(kernel, chips), out_shape=(jax.ShapeDtyp...]
    all_to_all x1 -> x0, blocking collectives: 187 us -> none  [body(): lax.all_to_all(send_rows, 'owner', split_axis=0, concat_axis=0, tiled=True)]
    all_to_all x3 -> x0, waiting for transfers between devices: 65.8 us -> none  [the longest x1 22.7 us: body(): lax.all_to_all(best, 'owner', split_axis=0, concat_axis=0, tiled=True)]
    all_to_all x3 -> x0, starting transfers between devices: 16 us -> none  [the longest x1 5.71 us: copy_for_each(): lax.all_to_all(jnp.broadcast_to(value[None], (length, *value.shape)), axi...]
    scatter x2 -> x0, local copies, waits for them, and re-layouts: 10.7 us -> none  [the longest x1 6.21 us: body(): jnp.zeros((slot_total, width), jnp.bfloat16).at[slot].set(embeddings)]
    another operation x3 -> x0, other arithmetic: 9.15 us -> none
    gather x1 -> x0, local copies, waits for them, and re-layouts: 8.83 us -> none  [body(): maxima = returned[slot]]
    dot_general x2 -> x0, matrix products: 4.5 us -> none  [rows_against(): jnp.dot(queries[first * width:(first + 1) * width], keys.T, preferred_ele...]
  transfers between devices with their start and end apart: 5 -> 0, of which waited for: 4 -> 0; matrix products, arithmetic and copies ran while one was open for 5% -> 0% of each run, Pallas kernels for 0% -> 0%
where the time goes in v1:
time: 210 us
  Pallas kernels  207 us (99%)
  local copies, waits for them, and re-layouts  2.48 us (1%)
    pallas_call x1, Pallas kernels, body(): pl.pallas_call(functools.partial(kernel, chips), out_shape=(jax.ShapeDtyp...  207 us

profile of v1, /device:TPU:37, one launch (start us, length us, event | category | flops | bytes accessed | tf_op | source)
XLA Modules:
  0.0 210.0 jit_solution(8019727335175166000)
XLA Ops:
  0.6 206.8 %shard_map.50 = (f32[1,1024]{1,0:T(1,128)}, f32[1,256]{1,0:T(1,128)}) custom-call(s32[1,1024]{1,0:T(1,128)} %bitcast.4, s32[1,256]{1,0:T(1,128)} %bitcast.7, bf16[1024,768]{1,0:T(8,128)(2,1)} %rows_ref.1), custom_call_target="tpu_custom_call" | custom-call | tf_op jit(solution)/shard_map/pallas_call | solution.py:250
  207.5 1.3 copy.7
  208.7 1.2 copy.8

commit v2 on v1

--- a/solution.py
+++ b/solution.py
@@ -10,7 +10,7 @@
 
 MESH = pl.DeviceIdType.MESH
 LANES = 128
-GROUPS = ((0, 16), (16, 24), (24, 28), (28, 32))
+GROUPS = ((0, 16), (16, 24), (24, 28))
 NT = (((1,), (1,)), ((), ()))
 TN = (((0,), (0,)), ((), ()))
 
@@ -27,15 +27,18 @@
     return lax.dot_general(a, b, dims, preferred_element_type=jnp.float32)
 
 
-def delta_of(pos, chips):
-    if pos == 0:
-        return 0
-    return (chips + 1 - pos) // 2 if pos % 2 else (pos + chips) // 2
-
-
-def place_of(delta, chips):
-    ahead = jnp.where(delta <= chips // 2, chips + 1 - 2 * delta, 2 * delta - chips)
-    return jnp.where(delta == 0, 0, ahead)
+def deltas(chips):
+    half, near = chips // 2, (2, 3, 4)
+    order = [0, *(d * way for d in near for way in (1, -1)), half]
+    far = [d for d in range(half - 1, 0, -1) if d not in near]
+    return order + [d * way for d in far for way in (1, -1)]
+
+
+def place_of(ahead, chips):
+    place = jnp.zeros_like(ahead)
+    for pos, delta in enumerate(deltas(chips)):
+        place = jnp.where(ahead == delta % chips, pos, place)
+    return place
 
 
 def three_parts(x):
@@ -47,9 +50,9 @@
 
 
 def kernel(
-    chips, ids_ref, map_ref, rows_ref, max_ref, mean_ref,
-    send, keys, lab_s, lab_r, lab_q, lab_k, acc, ret_s, ret_r, mp_s, mp_r, place, lane_at,
-    data_ss, data_rs, lab_ss, lab_rs, fwd_ss, fwd_rs, ret_ss, ret_rs, two_ss, two_rs,
+    chips, ids_hbm, map_hbm, rows_hbm, max_hbm, mean_hbm,
+    ids_ref, map_ref, rows_ref, max_ref, mean_ref, send, keys, lab_s, lab_r, lab_q, lab_k, acc, ret_s, ret_r, mp_s, mp_r, place, lane_at,
+    data_ss, data_rs, lab_ss, lab_rs, fwd_ss, fwd_rs, ret_ss, ret_rs, two_ss, two_rs, own_sem, known,
 ):
     items, width = rows_ref.shape
     clusters = map_ref.shape[1]
@@ -62,10 +65,31 @@
     def chip(delta):
         return {"owner": lax.rem(z + delta + 2 * chips, chips) * 2 + core}
 
+    def signal(semaphore, device):
+        pl.semaphore_signal(semaphore, inc=1, device_id=device, device_id_type=MESH)
+
+    ahead = deltas(chips)
     barrier = pltpu.get_barrier_semaphore()
-    for pos in range(1, chips):
-        pl.semaphore_signal(barrier, inc=1, device_id=chip(delta_of(pos, chips)), device_id_type=MESH)
-    pl.semaphore_signal(barrier, inc=1, device_id=partner, device_id_type=MESH)
+    for device in (chip(1), chip(-1), partner):
+        signal(barrier, device)
+    loads = [
+        pltpu.make_async_copy(source, target, own_sem.at[i])
+        for i, (source, target) in enumerate(((ids_hbm, ids_ref), (map_hbm, map_ref), (rows_hbm, rows_ref)))
+    ]
+    for load in loads:
+        load.start()
+
+    levels = math.ceil(math.log2(chips // 2))
+
+    def tell(level):
+        for way in (1, -1):
+            signal(known.at[level], chip(way * 2**level))
+
+    def learn(level):
+        pl.semaphore_wait(known.at[level], 2)
+
+    loads[0].wait()
+    loads[1].wait()
 
     pair_c = lax.shift_right_logical(map_ref[...], 1)
     place_c = place_of(lax.rem(pair_c - z + chips, chips), chips)
@@ -101,14 +125,14 @@
         return pltpu.make_async_remote_copy(
             src_ref=send.at[pl.ds(pos * block, block)], dst_ref=keys.at[pl.ds(pos * block, block)],
             send_sem=data_ss.at[pos], recv_sem=data_rs.at[pos],
-            device_id=chip(delta_of(pos, chips)), device_id_type=MESH,
+            device_id=chip(ahead[pos]), device_id_type=MESH,
         )
 
     def label_copy(pos):
         return pltpu.make_async_remote_copy(
             src_ref=lab_s.at[pos // per], dst_ref=lab_r.at[pos],
             send_sem=lab_ss.at[pos], recv_sem=lab_rs.at[pos],
-            device_id=chip(delta_of(pos, chips)), device_id_type=MESH,
+            device_id=chip(ahead[pos]), device_id_type=MESH,
         )
 
     def forward_copy(pos):
@@ -121,7 +145,7 @@
         return pltpu.make_async_remote_copy(
             src_ref=ret_s.at[pos], dst_ref=ret_r.at[pos],
             send_sem=ret_ss.at[pos], recv_sem=ret_rs.at[pos],
-            device_id=chip(-delta_of(pos, chips)), device_id_type=MESH,
+            device_id=chip(-ahead[pos]), device_id_type=MESH,
         )
 
     labels_over = pltpu.make_async_remote_copy(
@@ -134,7 +158,8 @@
     )
 
     step = 2 * LANES
-    for first in range(0, items, step):
+
+    def arrange(first):
         pick = jnp.where(iota((step, items), 0) + first == slot, 1.0, 0.0).astype(jnp.bfloat16)
         rows = product(pick, rows_ref[...])
         scale = lax.rsqrt(jnp.mean(rows * rows, axis=1, keepdims=True) + 1e-06)
@@ -146,11 +171,35 @@
         if first == 0:
             keys[:block] = unit[:block]
             lab_r[0] = names[:1, :LANES]
-            pl.semaphore_wait(barrier, chips)
-        for pos in range(first // block, (first + step) // block):
-            if pos > 0:
-                data_copy(pos).start()
-                label_copy(pos).start()
+
+    def start(copy, low, high):
+        for pos in range(1, chips):
+            if low <= abs(ahead[pos]) <= high:
+                copy(pos).start()
+
+    pl.semaphore_wait(barrier, 3)
+    tell(0)
+    loads[2].wait()
+    arrange(0)
+    learn(0)
+    tell(1)
+    start(label_copy, 2, 2)
+    start(data_copy, 2, 2)
+    arrange(step)
+    learn(1)
+    tell(2)
+    start(label_copy, 3, 4)
+    start(data_copy, 3, 4)
+    for first in range(2 * step, items, step):
+        arrange(first)
+    start(label_copy, 1, 1)
+    for level in range(2, levels):
+        learn(level)
+        if level + 1 < levels:
+            tell(level + 1)
+        start(label_copy, 2**level + 1, 2 ** (level + 1))
+    start(data_copy, 5, chips)
+    start(data_copy, 1, 1)
     forward_copy(0).start()
 
     for pos in range(1, chips):
@@ -166,36 +215,54 @@
         lab_k[t * LANES : (t + 1) * LANES] = jnp.broadcast_to(mixed, (LANES, LANES)).T
     acc[...] = jnp.full(acc.shape, -1.0, jnp.float32)
 
-    def meet(k0, kn, q0, qn, own):
-        gram = product(keys[pl.ds(k0, kn)], keys[q0 : q0 + qn], NT)
+    def best_of(gram, k0, q0, own):
+        kn, qn = gram.shape
         same = jnp.concatenate([lab_k[pl.ds(k0, kn)]] * (qn // LANES), axis=1) == lab_q[:, q0 : q0 + qn]
         if own:
             same = same & (iota((kn, qn), 0) + k0 != iota((kn, qn), 1) + q0)
-        best = jnp.where(same, gram, -1.0)
+        return jnp.where(same, gram, -1.0)
+
+    def meet(k0, kn, q0, qn, own):
+        best = best_of(product(keys[pl.ds(k0, kn)], keys[q0 : q0 + qn], NT), k0, q0, own)
         acc[:, q0 : q0 + qn] = jnp.maximum(acc[:, q0 : q0 + qn], jnp.max(best.reshape(kn // 8, 8, qn), axis=0))
+        return best
 
     def meet_all(k0, kn, q0, qn, own):
         size = math.gcd(kn, 2 * LANES)
-        if kn == size:
-            meet(k0, kn, q0, qn, own)
-        else:
-            @pl.loop(0, kn // size)
-            def _(i):
-                meet(pl.multiple_of(k0 + i * size, LANES), size, q0, qn, own)
-
-    for low, high in GROUPS:
+
+        @pl.loop(0, kn // size)
+        def _(i):
+            meet(pl.multiple_of(k0 + i * size, LANES), size, q0, qn, own)
+
+    def arrived(low, high):
         for pos in range(low, high):
             if pos > 0:
                 data_copy(pos).wait_recv()
                 forward_copy(pos).start()
+
+    def forwarded(low, high):
         for pos in range(low, high):
             forward_copy(pos).wait_recv()
+
+    for low, high in GROUPS:
+        arrived(low, high)
+        forwarded(low, high)
         old, new, end = low * block, (high - low) * block, high * block
         meet_all(old, new, 0, end, True)
         meet_all(items + old, new, 0, end, False)
         if old:
             meet_all(0, old, old, new, False)
             meet_all(items, old, old, new, False)
+    last = GROUPS[-1][1]
+    old, new = last * block, items - last * block
+    arrived(last, chips)
+    here = meet(old, new, 0, items, True)
+    there = best_of(product(keys[old:items], keys[items : items + old], NT), old, items, False)
+    column = jnp.maximum(jnp.max(here, axis=1, keepdims=True), jnp.max(there, axis=1, keepdims=True))
+    line = jnp.broadcast_to(column, (new, LANES)).T[:8]
+    acc[:, old:] = jnp.maximum(acc[:, old:], line)
+    forwarded(last, chips)
+    meet(items + old, new, 0, items, False)
 
     best = jnp.max(acc[...], axis=0, keepdims=True)
     kinds = 8
@@ -213,7 +280,7 @@
             ret_r[0] = packed
         else:
             ret_s[pos] = packed
-    for pos in range(1, chips):
+    for pos in sorted(range(1, chips), key=lambda pos: -abs(ahead[pos])):
         return_copy(pos).start()
 
     for pos in range(chips):
@@ -229,22 +296,32 @@
     for pos in range(1, chips):
         return_copy(pos).wait_recv()
     back = jnp.concatenate([ret_r[pos] for pos in range(chips)], axis=0)
-    values = product(jnp.concatenate(three_parts(back), axis=0), here, TN)
-    out = jnp.sum(jnp.where(wanted, values, 0.0), axis=0, keepdims=True)
-    mp_s[...] = out[:, items:]
+    back = jnp.concatenate(three_parts(back), axis=0)
+
+    def looked_up(low, high):
+        values = product(back, here[:, low:high], TN)
+        return jnp.sum(jnp.where(wanted[:, low:high], values, 0.0), axis=0, keepdims=True)
+
+    mp_s[...] = looked_up(items, total)
     means_over.start()
-    max_ref[...] = out[:, :items]
+    max_ref[...] = looked_up(0, items)
+    store_max = pltpu.make_async_copy(max_ref, max_hbm, own_sem.at[0])
+    store_max.start()
     for pos in range(1, chips):
         return_copy(pos).wait_send()
     means_over.wait()
     mean_ref[...] = mp_s[...] + mp_r[...]
+    store_mean = pltpu.make_async_copy(mean_ref, mean_hbm, own_sem.at[1])
+    store_mean.start()
+    store_max.wait()
+    store_mean.wait()
 
 
 def body(embeddings, cluster_ids, owner_map):
     chips = lax.axis_size("owner") // 2
     items, width = embeddings.shape
     clusters = owner_map.shape[0]
-    vmem = pl.BlockSpec(memory_space=pltpu.VMEM)
+    anywhere = pl.BlockSpec(memory_space=pl.ANY)
     row = (1, LANES)
     copies = [pltpu.SemaphoreType.DMA((chips,))] * 2
     maxima, means = pl.pallas_call(
@@ -253,9 +330,14 @@
             jax.ShapeDtypeStruct((1, items), jnp.float32),
             jax.ShapeDtypeStruct((1, clusters), jnp.float32),
         ),
-        in_specs=[vmem] * 3,
-        out_specs=(vmem, vmem),
+        in_specs=[anywhere] * 3,
+        out_specs=(anywhere, anywhere),
         scratch_shapes=[
+            pltpu.VMEM((1, items), jnp.int32),
+            pltpu.VMEM((1, clusters), jnp.int32),
+            pltpu.VMEM((items, width), jnp.bfloat16),
+            pltpu.VMEM((1, items), jnp.float32),
+            pltpu.VMEM((1, clusters), jnp.float32),
             pltpu.VMEM((items, width), jnp.bfloat16),
             pltpu.VMEM((2 * items, width), jnp.bfloat16),
             pltpu.VMEM((items // LANES, *row), jnp.float32),
@@ -271,6 +353,8 @@
             pltpu.VMEM((1, items + clusters), jnp.int32),
             *copies, *copies, *copies, *copies,
             *[pltpu.SemaphoreType.DMA((2,))] * 2,
+            pltpu.SemaphoreType.DMA((3,)),
+            pltpu.SemaphoreType.REGULAR((8,)),
         ],
         compiler_params=pltpu.CompilerParams(collective_id=0, has_side_effects=True),
     )(cluster_ids.reshape(1, items), owner_map.reshape(1, clusters), embeddings)

time: 210 us -> 188 us (0.90)
  Pallas kernels: 207 us -> 185 us
    pallas_call x1, Pallas kernels: 207 us -> 185 us  [body(): pl.pallas_call(functools.partial(kernel, chips), out_shape=(jax.ShapeDtyp...]
where the time goes in v2:
time: 188 us
  Pallas kernels  185 us (98%)
  local copies, waits for them, and re-layouts  2.48 us (1%)
    pallas_call x1, Pallas kernels, body(): pl.pallas_call(functools.partial(kernel, chips), out_shape=(jax.ShapeDtyp...  185 us

profile of v2, /device:TPU:37, one launch (start us, length us, event | category | flops | bytes accessed | tf_op | source)
XLA Modules:
  0.0 187.9 jit_solution(3314646413413917869)
XLA Ops:
  0.6 184.8 %shard_map.50 = (f32[1,1024]{1,0:T(1,128)}, f32[1,256]{1,0:T(1,128)}) custom-call(s32[1,1024]{1,0:T(1,128)} %bitcast.4, s32[1,256]{1,0:T(1,128)} %bitcast.7, bf16[1024,768]{1,0:T(8,128)(2,1)} %rows_hbm.1), custom_call_target="tpu_custom_call" | custom-call | tf_op jit(solution)/shard_map/pallas_call | solution.py:327
  185.4 1.3 copy.7
  186.7 1.2 copy.8

commit v3 on v2

--- a/solution.py
+++ b/solution.py
@@ -10,7 +10,8 @@
 
 MESH = pl.DeviceIdType.MESH
 LANES = 128
-GROUPS = ((0, 16), (16, 24), (24, 28))
+GROUPS = ((0, 16), (16, 24), (24, 28), (28, 32))
+LAST = 2
 NT = (((1,), (1,)), ((), ()))
 TN = (((0,), (0,)), ((), ()))
 
@@ -28,7 +29,7 @@
 
 
 def deltas(chips):
-    half, near = chips // 2, (2, 3, 4)
+    half, near = chips // 2, (2, 3, 4, 5)
     order = [0, *(d * way for d in near for way in (1, -1)), half]
     far = [d for d in range(half - 1, 0, -1) if d not in near]
     return order + [d * way for d in far for way in (1, -1)]
@@ -50,9 +51,9 @@
 
 
 def kernel(
-    chips, ids_hbm, map_hbm, rows_hbm, max_hbm, mean_hbm,
-    ids_ref, map_ref, rows_ref, max_ref, mean_ref, send, keys, lab_s, lab_r, lab_q, lab_k, acc, ret_s, ret_r, mp_s, mp_r, place, lane_at,
-    data_ss, data_rs, lab_ss, lab_rs, fwd_ss, fwd_rs, ret_ss, ret_rs, two_ss, two_rs, own_sem, known,
+    chips, ids_hbm, map_hbm, rows_hbm, out_hbm,
+    ids_ref, map_ref, rows_ref, out_ref, send, keys, lab_s, lab_r, lab_q, lab_k, acc, ret_s, ret_r, par_s, par_r, place, lane_at,
+    data_ss, data_rs, lab_ss, lab_rs, fwd_ss, fwd_rs, ret_ss, ret_rs, par_ss, par_rs, two_ss, two_rs, own_sem, known,
 ):
     items, width = rows_ref.shape
     clusters = map_ref.shape[1]
@@ -62,8 +63,11 @@
     core, z = lax.rem(me, 2), me // 2
     partner = {"owner": z * 2 + 1 - core}
 
-    def chip(delta):
-        return {"owner": lax.rem(z + delta + 2 * chips, chips) * 2 + core}
+    def chip(delta, which=core):
+        return {"owner": lax.rem(z + delta + 2 * chips, chips) * 2 + which}
+
+    def all_of(ref, semaphore):
+        pltpu.make_async_copy(ref, ref, semaphore).wait()
 
     def signal(semaphore, device):
         pl.semaphore_signal(semaphore, inc=1, device_id=device, device_id_type=MESH)
@@ -121,40 +125,47 @@
     lane_at[:, :items] = lax.rem(slot, LANES)
     lane_at[:, items:] = lax.rem(place_c + 1, per) * block + local_c.astype(jnp.int32)
 
+    group_of = {pos: g for g, (low, high) in enumerate(GROUPS) for pos in range(low, high)}
+
     def data_copy(pos):
         return pltpu.make_async_remote_copy(
             src_ref=send.at[pl.ds(pos * block, block)], dst_ref=keys.at[pl.ds(pos * block, block)],
-            send_sem=data_ss.at[pos], recv_sem=data_rs.at[pos],
+            send_sem=data_ss, recv_sem=data_rs.at[group_of[pos]],
             device_id=chip(ahead[pos]), device_id_type=MESH,
         )
 
     def label_copy(pos):
         return pltpu.make_async_remote_copy(
             src_ref=lab_s.at[pos // per], dst_ref=lab_r.at[pos],
-            send_sem=lab_ss.at[pos], recv_sem=lab_rs.at[pos],
+            send_sem=lab_ss, recv_sem=lab_rs,
             device_id=chip(ahead[pos]), device_id_type=MESH,
         )
 
-    def forward_copy(pos):
-        return pltpu.make_async_remote_copy(
-            src_ref=keys.at[pl.ds(pos * block, block)], dst_ref=keys.at[pl.ds(items + pos * block, block)],
-            send_sem=fwd_ss.at[pos], recv_sem=fwd_rs.at[pos], device_id=partner, device_id_type=MESH,
+    def forward_copy(g):
+        low, high = GROUPS[g]
+        return pltpu.make_async_remote_copy(
+            src_ref=keys.at[pl.ds(low * block, (high - low) * block)],
+            dst_ref=keys.at[pl.ds(items + low * block, (high - low) * block)],
+            send_sem=fwd_ss, recv_sem=fwd_rs.at[g], device_id=partner, device_id_type=MESH,
         )
 
     def return_copy(pos):
         return pltpu.make_async_remote_copy(
             src_ref=ret_s.at[pos], dst_ref=ret_r.at[pos],
-            send_sem=ret_ss.at[pos], recv_sem=ret_rs.at[pos],
+            send_sem=ret_ss, recv_sem=ret_rs,
             device_id=chip(-ahead[pos]), device_id_type=MESH,
+        )
+
+    def part_copy(pos):
+        return pltpu.make_async_remote_copy(
+            src_ref=par_s, dst_ref=par_r.at[pos],
+            send_sem=par_ss, recv_sem=par_rs,
+            device_id=chip(-ahead[pos], 1 - core), device_id_type=MESH,
         )
 
     labels_over = pltpu.make_async_remote_copy(
         src_ref=lab_r.at[pl.ds(0, chips)], dst_ref=lab_r.at[pl.ds(chips, chips)],
-        send_sem=two_ss.at[0], recv_sem=two_rs.at[0], device_id=partner, device_id_type=MESH,
-    )
-    means_over = pltpu.make_async_remote_copy(
-        src_ref=mp_s, dst_ref=mp_r,
-        send_sem=two_ss.at[1], recv_sem=two_rs.at[1], device_id=partner, device_id_type=MESH,
+        send_sem=two_ss, recv_sem=two_rs, device_id=partner, device_id_type=MESH,
     )
 
     step = 2 * LANES
@@ -181,16 +192,17 @@
     tell(0)
     loads[2].wait()
     arrange(0)
+    arrange(step)
     learn(0)
     tell(1)
     start(label_copy, 2, 2)
     start(data_copy, 2, 2)
-    arrange(step)
+    arrange(2 * step)
     learn(1)
     tell(2)
     start(label_copy, 3, 4)
     start(data_copy, 3, 4)
-    for first in range(2 * step, items, step):
+    for first in range(3 * step, items, step):
         arrange(first)
     start(label_copy, 1, 1)
     for level in range(2, levels):
@@ -198,12 +210,12 @@
         if level + 1 < levels:
             tell(level + 1)
         start(label_copy, 2**level + 1, 2 ** (level + 1))
-    start(data_copy, 5, chips)
+        if level == 2:
+            start(data_copy, 5, 5)
+    start(data_copy, 6, chips)
     start(data_copy, 1, 1)
-    forward_copy(0).start()
-
-    for pos in range(1, chips):
-        label_copy(pos).wait_recv()
+
+    all_of(lab_r.at[pl.ds(1, chips - 1)], lab_rs)
     labels_over.start()
     labels_over.wait_recv()
     quarter = lax.div(iota((1, LANES), 1), block)
@@ -234,34 +246,34 @@
         def _(i):
             meet(pl.multiple_of(k0 + i * size, LANES), size, q0, qn, own)
 
-    def arrived(low, high):
-        for pos in range(low, high):
-            if pos > 0:
-                data_copy(pos).wait_recv()
-                forward_copy(pos).start()
-
-    def forwarded(low, high):
-        for pos in range(low, high):
-            forward_copy(pos).wait_recv()
-
-    for low, high in GROUPS:
-        arrived(low, high)
-        forwarded(low, high)
+    def rows_of(g, ref):
+        low, high = GROUPS[g]
+        low = max(low, 1)
+        return ref.at[pl.ds(low * block, (high - low) * block)]
+
+    for g in range(LAST):
+        all_of(rows_of(g, keys), data_rs.at[g])
+        forward_copy(g).start()
+        forward_copy(g).wait_recv()
+        low, high = GROUPS[g]
         old, new, end = low * block, (high - low) * block, high * block
         meet_all(old, new, 0, end, True)
         meet_all(items + old, new, 0, end, False)
         if old:
             meet_all(0, old, old, new, False)
             meet_all(items, old, old, new, False)
-    last = GROUPS[-1][1]
-    old, new = last * block, items - last * block
-    arrived(last, chips)
+    old = GROUPS[LAST][0] * block
+    new = items - old
+    for g in range(LAST, len(GROUPS)):
+        all_of(rows_of(g, keys), data_rs.at[g])
+        forward_copy(g).start()
     here = meet(old, new, 0, items, True)
     there = best_of(product(keys[old:items], keys[items : items + old], NT), old, items, False)
     column = jnp.maximum(jnp.max(here, axis=1, keepdims=True), jnp.max(there, axis=1, keepdims=True))
     line = jnp.broadcast_to(column, (new, LANES)).T[:8]
     acc[:, old:] = jnp.maximum(acc[:, old:], line)
-    forwarded(last, chips)
+    for g in range(LAST, len(GROUPS)):
+        forward_copy(g).wait_recv()
     meet(items + old, new, 0, items, False)
 
     best = jnp.max(acc[...], axis=0, keepdims=True)
@@ -273,6 +285,7 @@
     part = jnp.sum(mine * best, axis=1, keepdims=True) / jnp.maximum(numbers, 1.0)
     spread = jnp.where(iota((kinds, LANES), 0) == lax.rem(iota((kinds, LANES), 1), kinds), part, 0.0)
     parts = jnp.sum(spread, axis=0, keepdims=True)
+    par_s[...] = parts
     for pos in range(chips):
         first = pos // per * LANES
         packed = jnp.where(quarter == pos % per, best[:, first : first + LANES], parts)
@@ -280,41 +293,45 @@
             ret_r[0] = packed
         else:
             ret_s[pos] = packed
-    for pos in sorted(range(1, chips), key=lambda pos: -abs(ahead[pos])):
-        return_copy(pos).start()
-
-    for pos in range(chips):
+    for pos in sorted(range(chips), key=lambda pos: -abs(ahead[pos])):
         if pos > 0:
-            data_copy(pos).wait_send()
-            label_copy(pos).wait_send()
-        forward_copy(pos).wait_send()
+            return_copy(pos).start()
+        part_copy(pos).start()
+    all_of(send.at[pl.ds(block, items - block)], data_ss)
+    all_of(keys.at[pl.ds(0, items)], fwd_ss)
+    all_of(lab_r.at[pl.ds(1, chips - 1)], lab_ss)
     labels_over.wait_send()
     total = items + clusters
     here = jnp.where(iota((chips, total), 0) == place[...], 1.0, 0.0).astype(jnp.bfloat16)
     here = jnp.concatenate([here] * 3, axis=0)
     wanted = iota((LANES, total), 0) == lane_at[...]
-    for pos in range(1, chips):
-        return_copy(pos).wait_recv()
-    back = jnp.concatenate([ret_r[pos] for pos in range(chips)], axis=0)
-    back = jnp.concatenate(three_parts(back), axis=0)
-
-    def looked_up(low, high):
-        values = product(back, here[:, low:high], TN)
+    all_of(ret_r.at[pl.ds(1, chips - 1)], ret_rs)
+    all_of(par_r, par_rs)
+
+    def looked_up(rows, low, high):
+        rows = jnp.concatenate(three_parts(jnp.concatenate(rows, axis=0)), axis=0)
+        values = product(rows, here[:, low:high], TN)
         return jnp.sum(jnp.where(wanted[:, low:high], values, 0.0), axis=0, keepdims=True)
 
-    mp_s[...] = looked_up(items, total)
-    means_over.start()
-    max_ref[...] = looked_up(0, items)
-    store_max = pltpu.make_async_copy(max_ref, max_hbm, own_sem.at[0])
-    store_max.start()
-    for pos in range(1, chips):
-        return_copy(pos).wait_send()
-    means_over.wait()
-    mean_ref[...] = mp_s[...] + mp_r[...]
-    store_mean = pltpu.make_async_copy(mean_ref, mean_hbm, own_sem.at[1])
-    store_mean.start()
-    store_max.wait()
-    store_mean.wait()
+    out_ref[:, items:] = looked_up([ret_r[pos] + par_r[pos] for pos in range(chips)], items, total)
+    out_ref[:, :items] = looked_up([ret_r[pos] for pos in range(chips)], 0, items)
+    store = pltpu.make_async_copy(out_ref, out_hbm, own_sem.at[0])
+    store.start()
+    all_of(ret_r.at[pl.ds(1, chips - 1)], ret_ss)
+    all_of(par_r, par_ss)
+    store.wait()
+
+
+def split(out_hbm, max_hbm, mean_hbm, sem):
+    items = max_hbm.shape[1]
+    copies = [
+        pltpu.make_async_copy(out_hbm.at[:, pl.ds(0, items)], max_hbm, sem.at[0]),
+        pltpu.make_async_copy(out_hbm.at[:, pl.ds(items, mean_hbm.shape[1])], mean_hbm, sem.at[1]),
+    ]
+    for copy in copies:
+        copy.start()
+    for copy in copies:
+        copy.wait()
 
 
 def body(embeddings, cluster_ids, owner_map):
@@ -323,21 +340,17 @@
     clusters = owner_map.shape[0]
     anywhere = pl.BlockSpec(memory_space=pl.ANY)
     row = (1, LANES)
-    copies = [pltpu.SemaphoreType.DMA((chips,))] * 2
-    maxima, means = pl.pallas_call(
+    dma = pltpu.SemaphoreType.DMA
+    both = pl.pallas_call(
         functools.partial(kernel, chips),
-        out_shape=(
-            jax.ShapeDtypeStruct((1, items), jnp.float32),
-            jax.ShapeDtypeStruct((1, clusters), jnp.float32),
-        ),
+        out_shape=jax.ShapeDtypeStruct((1, items + clusters), jnp.float32),
         in_specs=[anywhere] * 3,
-        out_specs=(anywhere, anywhere),
+        out_specs=anywhere,
         scratch_shapes=[
             pltpu.VMEM((1, items), jnp.int32),
             pltpu.VMEM((1, clusters), jnp.int32),
             pltpu.VMEM((items, width), jnp.bfloat16),
-            pltpu.VMEM((1, items), jnp.float32),
-            pltpu.VMEM((1, clusters), jnp.float32),
+            pltpu.VMEM((1, items + clusters), jnp.float32),
             pltpu.VMEM((items, width), jnp.bfloat16),
             pltpu.VMEM((2 * items, width), jnp.bfloat16),
             pltpu.VMEM((items // LANES, *row), jnp.float32),
@@ -347,17 +360,26 @@
             pltpu.VMEM((8, items), jnp.float32),
             pltpu.VMEM((chips, *row), jnp.float32),
             pltpu.VMEM((chips, *row), jnp.float32),
-            pltpu.VMEM((1, clusters), jnp.float32),
-            pltpu.VMEM((1, clusters), jnp.float32),
+            pltpu.VMEM(row, jnp.float32),
+            pltpu.VMEM((chips, *row), jnp.float32),
             pltpu.VMEM((1, items + clusters), jnp.int32),
             pltpu.VMEM((1, items + clusters), jnp.int32),
-            *copies, *copies, *copies, *copies,
-            *[pltpu.SemaphoreType.DMA((2,))] * 2,
-            pltpu.SemaphoreType.DMA((3,)),
-            pltpu.SemaphoreType.REGULAR((8,)),
+            dma, dma((len(GROUPS),)), dma, dma, dma, dma((len(GROUPS),)),
+            dma, dma, dma, dma, dma, dma, dma((3,)),
+            pltpu.SemaphoreType.REGULAR((4,)),
         ],
         compiler_params=pltpu.CompilerParams(collective_id=0, has_side_effects=True),
     )(cluster_ids.reshape(1, items), owner_map.reshape(1, clusters), embeddings)
+    maxima, means = pl.pallas_call(
+        split,
+        out_shape=(
+            jax.ShapeDtypeStruct((1, items), jnp.float32),
+            jax.ShapeDtypeStruct((1, clusters), jnp.float32),
+        ),
+        in_specs=[anywhere],
+        out_specs=(anywhere, anywhere),
+        scratch_shapes=[dma((2,))],
+    )(both)
     return maxima.reshape(items), means.reshape(clusters)
 
 

time: 188 us -> 181 us (0.963)
  Pallas kernels: 185 us -> 180 us
  local copies, waits for them, and re-layouts: 2.48 us -> 0 us
    pallas_call x1 -> x2, Pallas kernels: 185 us -> 180 us  [the longest x1 179 us: body(): pl.pallas_call(functools.partial(kernel, chips), out_shape=jax.ShapeDtype...]
    unnamed x2 -> x0, local copies, waits for them, and re-layouts: 2.48 us -> none
where the time goes in v3:
time: 181 us
  Pallas kernels  180 us (99%)
    pallas_call x1, Pallas kernels, body(): pl.pallas_call(functools.partial(kernel, chips), out_shape=jax.ShapeDtype...  179 us

profile of v3, /device:TPU:37, one launch (start us, length us, event | category | flops | bytes accessed | tf_op | source)
XLA Modules:
  0.0 180.5 jit_solution(5821060309931329632)
XLA Ops:
  0.6 178.6 %shard_map.50.out_hbm = f32[1,1280]{1,0:T(1,128)} custom-call(s32[1,1024]{1,0:T(1,128)} %bitcast.4, s32[1,256]{1,0:T(1,128)} %bitcast.5, bf16[1024,768]{1,0:T(8,128)(2,1)} %rows_hbm.1), custom_call_target="tpu_custom_call" | custom-call | tf_op jit(solution)/shard_map/pallas_call | solution.py:344
  179.3 1.3 shard_map.51

commit v4 on v3

--- a/solution.py
+++ b/solution.py
@@ -92,6 +92,8 @@
     def learn(level):
         pl.semaphore_wait(known.at[level], 2)
 
+    pl.semaphore_wait(barrier, 3)
+    tell(0)
     loads[0].wait()
     loads[1].wait()
 
@@ -188,21 +190,18 @@
             if low <= abs(ahead[pos]) <= high:
                 copy(pos).start()
 
-    pl.semaphore_wait(barrier, 3)
-    tell(0)
     loads[2].wait()
     arrange(0)
-    arrange(step)
     learn(0)
     tell(1)
+    start(data_copy, 2, 2)
     start(label_copy, 2, 2)
-    start(data_copy, 2, 2)
-    arrange(2 * step)
+    arrange(step)
     learn(1)
     tell(2)
+    start(data_copy, 3, 4)
     start(label_copy, 3, 4)
-    start(data_copy, 3, 4)
-    for first in range(3 * step, items, step):
+    for first in range(2 * step, items, step):
         arrange(first)
     start(label_copy, 1, 1)
     for level in range(2, levels):
@@ -368,8 +367,11 @@
             dma, dma, dma, dma, dma, dma, dma((3,)),
             pltpu.SemaphoreType.REGULAR((4,)),
         ],
-        compiler_params=pltpu.CompilerParams(collective_id=0, has_side_effects=True),
-    )(cluster_ids.reshape(1, items), owner_map.reshape(1, clusters), embeddings)
+        compiler_params=pltpu.CompilerParams(collective_id=0, has_side_effects=True, vmem_limit_bytes=32 * 2**20),
+    )(*[
+        pltpu.with_memory_space_constraint(array, pltpu.HBM)
+        for array in (cluster_ids.reshape(1, items), owner_map.reshape(1, clusters), embeddings)
+    ])
     maxima, means = pl.pallas_call(
         split,
         out_shape=(
@@ -379,6 +381,7 @@
         in_specs=[anywhere],
         out_specs=(anywhere, anywhere),
         scratch_shapes=[dma((2,))],
+        compiler_params=pltpu.CompilerParams(vmem_limit_bytes=2**20),
     )(both)
     return maxima.reshape(items), means.reshape(clusters)
 

time: 181 us -> 179 us (0.989)
  no operation moved by 1% of the time
where the time goes in v4:
time: 179 us
  Pallas kernels  179 us (100%)
    pallas_call x1, Pallas kernels, body(): pl.pallas_call(functools.partial(kernel, chips), out_shape=jax.ShapeDtype...  178 us

profile of v4, /device:TPU:37, one launch (start us, length us, event | category | flops | bytes accessed | tf_op | source)
XLA Modules:
  0.0 179.4 jit_solution(12623301459711289296)
XLA Ops:
  0.6 178.1 %shard_map.50.out_hbm = f32[1,1280]{1,0:T(1,128)S(1)} custom-call(s32[1,1024]{1,0:T(1,128)} %bitcast.4, s32[1,256]{1,0:T(1,128)} %bitcast.5, bf16[1024,768]{1,0:T(8,128)(2,1)} %rows_hbm.1), custom_call_target="tpu_custom_call" | custom-call | tf_op jit(solution)/shard_map/pallas_call | solution.py:343
  178.8 0.6 shard_map.51

commit v5 on v4

--- a/solution.py
+++ b/solution.py
@@ -203,13 +203,13 @@
     start(label_copy, 3, 4)
     for first in range(2 * step, items, step):
         arrange(first)
-    start(label_copy, 1, 1)
     for level in range(2, levels):
         learn(level)
         if level + 1 < levels:
             tell(level + 1)
         start(label_copy, 2**level + 1, 2 ** (level + 1))
         if level == 2:
+            start(label_copy, 1, 1)
             start(data_copy, 5, 5)
     start(data_copy, 6, chips)
     start(data_copy, 1, 1)

time: 179 us -> 180 us (level)
  no operation moved by 1% of the time
where the time goes in v5:
time: 180 us; the launch traced here: 179 us
  Pallas kernels  179 us (99%)
    pallas_call x1, Pallas kernels, body(): pl.pallas_call(functools.partial(kernel, chips), out_shape=jax.ShapeDtype...  178 us

profile of v5, /device:TPU:37, one launch (start us, length us, event | category | flops | bytes accessed | tf_op | source)
XLA Modules:
  0.0 179.5 jit_solution(2295509097719904549)
XLA Ops:
  0.6 178.2 %shard_map.50.out_hbm = f32[1,1280]{1,0:T(1,128)S(1)} custom-call(s32[1,1024]{1,0:T(1,128)} %bitcast.4, s32[1,256]{1,0:T(1,128)} %bitcast.5, bf16[1024,768]{1,0:T(8,128)(2,1)} %rows_hbm.1), custom_call_target="tpu_custom_call" | custom-call | tf_op jit(solution)/shard_map/pallas_call | solution.py:343
  178.9 0.6 shard_map.51
